TPU v7x, 32 devices: a whole 2x2x4 slice. The times are simulated.
32 devices in a mesh: seq: 4 (over z), wt: 8 (over y, x, core).
Axes of the slice: x: 2, y: 2, z: 4, core: 2. Of those that a mesh axis runs over, the one named last changes fastest.
Arguments:
- tokens: bfloat16 [8, 512, 2048], P('wt', 'seq'), may hold values from -6 to 6
- cotangent: bfloat16 [8, 512, 2048], P('wt', 'seq'), may hold values from -6 to 6
- segment_ids: int32 [8, 512], P('wt'), may hold values from 0 to 1, never falling along the last dimension, each value on 1 to 320 neighbouring positions
- expert_routes: int32 [8, 512, 8], P('wt', 'seq'), may hold values from 0 to 15, all different within a row; in each aligned block of 128 rows (0 to 127, 128 to 255, ..., all dimensions but the last counted through in order) at most 128 rows name the same one
- w_qkv: bfloat16 [2048, 6144], P('wt'), may hold values from -0.125 to 0.125
- w_out: bfloat16 [2048, 2048], P('wt'), may hold values from -2 to 2
- w_router: bfloat16 [2048, 16], P('wt'), may hold values from -0.0625 to 0.0625
- w_gate_up: bfloat16 [16, 2048, 2048], P('seq', 'wt'), may hold values from -0.125 to 0.125
- w_down: bfloat16 [16, 1024, 2048], P('seq', 'wt'), may hold values from -0.75 to 0.75
- attn_gain: bfloat16 [2048], P('wt'), may hold values from 0.5 to 1.5
- ffn_gain: bfloat16 [2048], P('wt'), may hold values from 0.5 to 1.5
- q_gain: bfloat16 [128], P('wt'), may hold values from 0.5 to 1.5
- k_gain: bfloat16 [128], P('wt'), may hold values from 0.5 to 1.5
Outputs:
- output: bfloat16 [8, 512, 2048], P('wt', 'seq')
- tokens_grad: float32 [8, 512, 2048], P('wt', 'seq')
- w_qkv_grad: float32 [2048, 6144], P('wt')
- w_out_grad: float32 [2048, 2048], P('wt')
- w_router_grad: float32 [2048, 16], P('wt')
- w_gate_up_grad: float32 [16, 2048, 2048], P('seq', 'wt')
- w_down_grad: float32 [16, 1024, 2048], P('seq', 'wt')
- attn_gain_grad: float32 [2048], P('wt')
- ffn_gain_grad: float32 [2048], P('wt')
- q_gain_grad: float32 [128], P('wt')
- k_gain_grad: float32 [128], P('wt')
Inputs may be any that keep to these rules, and one draw needn't show every extreme that they name: `segment_ids`: along a sequence the segment numbers never fall; each of the 2 documents spans 1 to 320 positions. `expert_routes`: A token names 8 different experts; among the 128 tokens of one device no expert is named more than 128 times, a bound that some block reaches.
All inputs are finite; a program needn't handle non-finite values.
Results may differ from a plain program's by a relative error of at most 0.028.
Values may be sent and summed in bfloat16 or wider, within the bound.
A program may use at most 512 MiB of HBM per device.

v0:
```python
import jax
import jax.numpy as jnp
import numpy as np
from jax import lax
from jax.sharding import PartitionSpec as P

H = 16
HD = 128
FF = 1024
EPS = 1e-06
THETA = 50000.0
NEG = -1e30
LANES = 128
BF = jnp.bfloat16
F32 = jnp.float32


def normalize(values):
    factor = lax.rsqrt(jnp.mean(values * values, axis=-1, keepdims=True) + EPS)
    return (values * factor, factor)


def norm_back(grad_normed, normed_values, factor):
    return factor * (
        grad_normed - normed_values * jnp.mean(grad_normed * normed_values, axis=-1, keepdims=True)
    )


def rope_tables(length):
    half = HD // 2
    freq = THETA ** (-jnp.arange(half, dtype=F32) * 2.0 / HD)
    angle = jnp.arange(length, dtype=F32)[:, None] * freq[None, :]
    return (jnp.cos(angle)[:, None, :], jnp.sin(angle)[:, None, :])


def rotate(values, cosine, sine):
    half = values.shape[-1] // 2
    first = values[..., :half]
    second = values[..., half:]
    return jnp.concatenate(
        [first * cosine - second * sine, second * cosine + first * sine], axis=-1
    )


def dot(left, right, dims):
    return lax.dot_general(left, right, (dims, ((), ())), preferred_element_type=F32)


def nn(left, right):
    return dot(left, right, ((1,), (0,)))


def nt(left, right):
    return dot(left, right, ((1,), (1,)))


def tn(left, right):
    return dot(left, right, ((0,), (0,)))


def split_two(values):
    high = values.astype(BF)
    low = (values - high.astype(F32)).astype(BF)
    return (high, low)


def body(
    tokens,
    cotangent,
    segment_ids,
    expert_routes,
    w_qkv,
    w_out,
    w_router,
    w_gate_up,
    w_down,
    attn_gain,
    ffn_gain,
    q_gain,
    k_gain,
):
    seq_total = lax.axis_size("seq")
    wt_total = lax.axis_size("wt")
    seq_me = lax.axis_index("seq")
    rows = tokens.shape[1]
    model = tokens.shape[2]
    length = rows * seq_total
    shard = w_qkv.shape[0]
    local_experts = w_gate_up.shape[0]
    experts = w_router.shape[1]
    heads = H // seq_total
    cols = 3 * heads * HD
    gain_part = q_gain.shape[0]
    tokens_all = lax.all_gather(tokens[0], "seq", axis=0, tiled=True)
    routes_all = lax.all_gather(expert_routes[0], "seq", axis=0, tiled=True)
    w_here = lax.dynamic_slice_in_dim(
        w_qkv.reshape(shard, 3, seq_total, heads * HD), seq_me, 1, axis=2
    ).reshape(shard, cols)
    small = jnp.concatenate(
        [
            w_router,
            attn_gain[:, None],
            ffn_gain[:, None],
            jnp.pad(q_gain, (0, shard - gain_part))[:, None],
            jnp.pad(k_gain, (0, shard - gain_part))[:, None],
        ],
        axis=1,
    )
    small = jnp.pad(small, ((0, 0), (0, LANES - small.shape[1])))
    qkv_full = lax.all_gather(jnp.concatenate([w_here, small], axis=1), "wt", axis=0, tiled=True)
    out_full = lax.all_gather(w_out, "wt", axis=0, tiled=True)
    grad_all = lax.all_gather(cotangent[0], "seq", axis=0, tiled=True)
    expert_full = [
        lax.all_gather(jnp.concatenate([w_gate_up[e], w_down[e]], axis=0), "wt", axis=0)
        for e in range(local_experts)
    ]
    small_full = qkv_full[:, cols:]
    router_full = small_full[:, :experts]
    picker = np.zeros((8, LANES), np.float32)
    for row in range(4):
        picker[row, experts + row] = 1.0
    gain_rows = nt(jnp.asarray(picker, BF), small_full)
    gain_attn = gain_rows[0]
    gain_ffn = gain_rows[1]
    gain_query = gain_rows[2].reshape(wt_total, shard)[:, :gain_part].reshape(HD)
    gain_key = gain_rows[3].reshape(wt_total, shard)[:, :gain_part].reshape(HD)
    segments = segment_ids[0]
    same = segments[:, None] == segments[None, :]
    cosine, sine = rope_tables(length)
    normed_all, _ = normalize(tokens_all.astype(F32))
    hidden = (normed_all * gain_attn).astype(BF)
    projected = nn(hidden, qkv_full)[:, :cols].reshape(length, 3, heads, HD)
    normed_q, factor_q = normalize(projected[:, 0])
    normed_k, factor_k = normalize(projected[:, 1])
    queries = jnp.swapaxes(rotate(normed_q * gain_query, cosine, sine).astype(BF), 0, 1)
    keys = jnp.swapaxes(rotate(normed_k * gain_key, cosine, sine).astype(BF), 0, 1)
    values = jnp.swapaxes(projected[:, 2].astype(BF), 0, 1)
    scale = HD ** (-0.5)

    def bmm(left, right, dims):
        return lax.dot_general(left, right, (dims, ((0,), (0,))), preferred_element_type=F32)

    logits = jnp.where(same[None], bmm(queries, keys, ((2,), (2,))) * scale, NEG)
    powers = jnp.exp(logits - jnp.max(logits, axis=-1, keepdims=True))
    weights = powers / jnp.sum(powers, axis=-1, keepdims=True)
    weights_low = weights.astype(BF)
    attended = bmm(weights_low, values, ((2,), (1,))).astype(BF)
    merged = lax.all_to_all(
        jnp.swapaxes(attended, 0, 1), "seq", split_axis=0, concat_axis=1, tiled=True
    ).reshape(rows, H * HD)
    inputs = tokens[0].astype(F32)
    residual = inputs + nn(merged, out_full)
    normed_f, factor_f = normalize(residual)
    hidden_own = (normed_f * gain_ffn).astype(BF)
    hidden_ffn = lax.all_gather(hidden_own, "seq", axis=0, tiled=True)
    chances = jax.nn.softmax(nn(hidden_ffn, router_full), axis=-1)
    expert_ids = jnp.arange(experts, dtype=jnp.int32)
    routed = jnp.any(routes_all[:, :, None] == expert_ids[None, None, :], axis=1)
    picked = jnp.where(routed, chances, 0.0)
    picked_total = jnp.sum(picked, axis=1, keepdims=True)
    gates = picked / picked_total
    gates_here = lax.dynamic_slice_in_dim(gates, seq_me * local_experts, local_experts, axis=1)
    out_part = jnp.zeros((length, model), F32)
    grad_hidden_part = jnp.zeros((length, model), F32)
    gate_grads = []
    expert_grads = []
    for e in range(local_experts):
        gate = gates_here[:, e : e + 1]
        gate_up = expert_full[e][:, : model // wt_total].reshape(model, 2 * FF)
        down = expert_full[e][:, model // wt_total :].reshape(FF, model)
        before = nn(hidden_ffn, gate_up)
        gate_part = before[:, :FF]
        up_part = before[:, FF:]
        sigmoid_gate = jax.nn.sigmoid(gate_part)
        silu_gate = gate_part * sigmoid_gate
        activated = silu_gate * up_part
        scaled = (gate * activated).astype(BF)
        grad_act = nt(grad_all, down)
        gate_grads.append(jnp.sum(grad_act * activated, axis=1, keepdims=True))
        grad_act = grad_act * gate
        grad_gate = grad_act * up_part * sigmoid_gate * (1.0 + gate_part * (1.0 - sigmoid_gate))
        grad_up = grad_act * silu_gate
        grad_before = jnp.concatenate([grad_gate, grad_up], axis=-1).astype(BF)
        out_part = out_part + nn(scaled, down)
        grad_hidden_part = grad_hidden_part + nt(grad_before, gate_up)
        gate_up_grad = tn(hidden_ffn, grad_before).astype(BF)
        down_grad = tn(scaled, grad_all).astype(BF)
        joined = jnp.concatenate(
            [
                gate_up_grad.reshape(wt_total, model // wt_total, 2 * FF),
                down_grad.reshape(wt_total, FF // wt_total, model),
            ],
            axis=1,
        )
        expert_grads.append(
            lax.psum_scatter(joined, "wt", scatter_dimension=0, tiled=False).astype(F32)
        )
    gate_up_out = jnp.stack([g[: model // wt_total] for g in expert_grads])
    down_out = jnp.stack([g[model // wt_total :] for g in expert_grads])
    gate_grad_part = jnp.concatenate(gate_grads, axis=1)
    gate_high, gate_low = split_two(gate_grad_part)

    def spread(part):
        wide = jnp.zeros((length, experts), BF)
        return lax.dynamic_update_slice(wide, part, (0, seq_me * local_experts))

    returned = lax.psum_scatter(
        jnp.concatenate([grad_hidden_part.astype(BF), spread(gate_high), spread(gate_low)], axis=1),
        "seq",
        scatter_dimension=0,
        tiled=True,
    ).astype(F32)
    grad_hidden = returned[:, :model]
    gate_grad = returned[:, model : model + experts] + returned[:, model + experts :]
    moe_out = lax.psum_scatter(out_part.astype(BF), "seq", scatter_dimension=0, tiled=True).astype(
        F32
    )
    output = (residual + moe_out).astype(BF)

    def own(full):
        return lax.dynamic_slice_in_dim(full, seq_me * rows, rows, axis=0)

    chances_own = own(chances)
    routed_own = own(routed)
    gates_own = own(gates)
    inner_gate = jnp.sum(gate_grad * gates_own, axis=1, keepdims=True)
    grad_chances = jnp.where(routed_own, (gate_grad - inner_gate) / own(picked_total), 0.0)
    grad_logits = (
        chances_own * (grad_chances - jnp.sum(grad_chances * chances_own, axis=1, keepdims=True))
    ).astype(BF)
    grad_hidden = grad_hidden + nt(grad_logits, router_full)
    router_grad = tn(hidden_own, grad_logits)
    ffn_gain_grad = jnp.sum(grad_hidden * normed_f, axis=0)
    grad_residual = cotangent[0].astype(F32) + norm_back(grad_hidden * gain_ffn, normed_f, factor_f)
    grad_branch = grad_residual.astype(BF)
    grad_merged = nt(grad_branch, out_full).astype(BF).reshape(rows, H, HD)
    grad_heads = jnp.swapaxes(
        lax.all_to_all(grad_merged, "seq", split_axis=1, concat_axis=0, tiled=True), 0, 1
    )
    out_grad = lax.psum_scatter(
        tn(merged, grad_branch).astype(BF), "wt", scatter_dimension=0, tiled=True
    )
    out_grad = lax.psum(out_grad, "seq").astype(F32)
    grad_weights = bmm(grad_heads, values, ((2,), (2,)))
    inner = jnp.sum(weights * grad_weights, axis=-1, keepdims=True)
    grad_scores = (weights * (grad_weights - inner)).astype(BF)
    grad_q = jnp.swapaxes(bmm(grad_scores, keys, ((2,), (1,))), 0, 1) * scale
    grad_k = jnp.swapaxes(bmm(grad_scores, queries, ((1,), (1,))), 0, 1) * scale
    grad_v = jnp.swapaxes(bmm(weights_low, grad_heads, ((1,), (1,))), 0, 1)
    grad_q_normed = rotate(grad_q, cosine, -sine)
    grad_k_normed = rotate(grad_k, cosine, -sine)
    q_gain_grad = jnp.sum(grad_q_normed * normed_q, axis=(0, 1))
    k_gain_grad = jnp.sum(grad_k_normed * normed_k, axis=(0, 1))
    grad_q_raw = norm_back(grad_q_normed * gain_query, normed_q, factor_q)
    grad_k_raw = norm_back(grad_k_normed * gain_key, normed_k, factor_k)
    grad_projected = (
        jnp.stack([grad_q_raw, grad_k_raw, grad_v], axis=1).reshape(length, cols).astype(BF)
    )
    qkv_grad = tn(hidden, grad_projected)
    grad_normed_part = nt(jnp.pad(grad_projected, ((0, 0), (0, LANES))), qkv_full)
    attn_gain_grad = jnp.sum(grad_normed_part * normed_all, axis=0)
    grad_normed_own = lax.psum_scatter(
        grad_normed_part.astype(BF), "seq", scatter_dimension=0, tiled=True
    ).astype(F32)
    normed_a, factor_a = normalize(inputs)
    tokens_grad = grad_residual + norm_back(grad_normed_own * gain_attn, normed_a, factor_a)

    def gain_column(vector):
        return jnp.pad(
            vector.reshape(wt_total, gain_part), ((0, 0), (0, shard - gain_part))
        ).reshape(model, 1)

    small_grad = jnp.concatenate(
        [
            router_grad,
            attn_gain_grad[:, None],
            ffn_gain_grad[:, None],
            gain_column(q_gain_grad),
            gain_column(k_gain_grad),
        ],
        axis=1,
    )
    small_grad = jnp.pad(small_grad, ((0, 0), (0, LANES - small_grad.shape[1])))
    scattered = lax.psum_scatter(
        jnp.concatenate([qkv_grad, small_grad], axis=1).astype(BF),
        "wt",
        scatter_dimension=0,
        tiled=True,
    )
    collected = lax.all_gather(scattered, "seq", axis=0).astype(F32)
    qkv_out = (
        collected[:, :, :cols]
        .reshape(seq_total, shard, 3, heads * HD)
        .transpose(1, 2, 0, 3)
        .reshape(shard, 3 * H * HD)
    )
    small_out = jnp.sum(collected[:, :, cols:], axis=0)
    return (
        output[None],
        tokens_grad[None],
        qkv_out,
        out_grad,
        small_out[:, :experts],
        gate_up_out,
        down_out,
        small_out[:, experts],
        small_out[:, experts + 1],
        small_out[:gain_part, experts + 2],
        small_out[:gain_part, experts + 3],
    )


def solution(mesh):
    in_specs = (
        P("wt", "seq", None),
        P("wt", "seq", None),
        P("wt", None),
        P("wt", "seq", None),
        P("wt", None),
        P("wt", None),
        P("wt", None),
        P("seq", "wt", None),
        P("seq", "wt", None),
        P("wt"),
        P("wt"),
        P("wt"),
        P("wt"),
    )
    out_specs = (
        P("wt", "seq", None),
        P("wt", "seq", None),
        P("wt", None),
        P("wt", None),
        P("wt", None),
        P("seq", "wt", None),
        P("seq", "wt", None),
        P("wt"),
        P("wt"),
        P("wt"),
        P("wt"),
    )
    return jax.shard_map(body, mesh=mesh, in_specs=in_specs, out_specs=out_specs, check_vma=False)
```

profile of v0, /device:TPU:0, one launch (start us, length us, event | category | flops | bytes accessed | tf_op | source)
XLA Modules:
  0.0 1457.3 jit_solution(14407658807051301885)
XLA Ops:
  18.4 39.6 %all-gather.25.cloned.1.call-done = bf16[1,512,2048]{2,1,0:T(8,128)(2,1)} async-done(((bf16[1,128,2048]{2,1,0:T(8,128)(2,1)}), bf16[1,512,2048]{2,1,0:T(8,128)(2,1)}) %all-gather.25.cloned.1.call-update) | async-done | bytes 2097168 | tf_op jit(solution)/shard_map/all_gather | solution.py:94
  60.1 48.1 %all-gather.19.cloned.1.call-done = bf16[2048,1664]{0,1:T(8,128)(2,1)} async-done(((bf16[256,1664]{0,1:T(8,128)(2,1)}), bf16[2048,1664]{0,1:T(8,128)(2,1)}) %all-gather.19.cloned.1.call-update) | async-done | bytes 6815760 | tf_op jit(solution)/shard_map/all_gather | solution.py:110
  110.0 8.6 fusion.3
  133.7 19.4 %all_to_all.33 = bf16[512,4,128]{2,1,0:T(4,128)(2,1)S(1)} all-to-all(bf16[512,4,128]{2,1,0:T(4,128)(2,1)S(1)} %copy.163), channel_id=1, replica_groups=mesh['seq'=4,'wt'=8] {'seq'}, dimensions={0} | all-to-all | bytes 1048576 | tf_op jit(solution)/shard_map/all_to_all | solution.py:148
  153.4 10.9 all-gather.21.cloned.1.call-done
  182.9 13.9 all-gather.1
  197.0 20.3 %all-gather.23.cloned.1.call-done = bf16[512,2048]{1,0:T(8,128)(2,1)} async-done(((bf16[128,2048]{1,0:T(8,128)(2,1)}), bf16[512,2048]{1,0:T(8,128)(2,1)}) %all-gather.23.cloned.1.call-update) | async-done | bytes 2097168 | tf_op jit(solution)/shard_map/all_gather | solution.py:155
  222.4 68.0 %all-gather.31.cloned.1.call-done = bf16[3072,2048]{1,0:T(8,128)(2,1)} async-done(((bf16[384,2048]{1,0:T(8,128)(2,1)}), bf16[3072,2048]{1,0:T(8,128)(2,1)}) %all-gather.31.cloned.1.call-update) | async-done | bytes 12582928 | tf_op jit(solution)/shard_map/all_gather | solution.py:114
  304.3 60.5 %all-gather.27.cloned.1.call-done = bf16[3072,2048]{1,0:T(8,128)(2,1)} async-done(((bf16[384,2048]{1,0:T(8,128)(2,1)}), bf16[3072,2048]{1,0:T(8,128)(2,1)}) %all-gather.27.cloned.1.call-update) | async-done | bytes 12582928 | tf_op jit(solution)/shard_map/all_gather | solution.py:114
  378.5 60.2 %all-gather.29.cloned.1.call-done = bf16[3072,2048]{1,0:T(8,128)(2,1)} async-done(((bf16[384,2048]{1,0:T(8,128)(2,1)}), bf16[3072,2048]{1,0:T(8,128)(2,1)}) %all-gather.29.cloned.1.call-update) | async-done | bytes 12582928 | tf_op jit(solution)/shard_map/all_gather | solution.py:114
  452.5 60.1 %all-gather.33.cloned.1.call-done = bf16[3072,2048]{1,0:T(8,128)(2,1)} async-done(((bf16[384,2048]{1,0:T(8,128)(2,1)}), bf16[3072,2048]{1,0:T(8,128)(2,1)}) %all-gather.33.cloned.1.call-update) | async-done | bytes 12582928 | tf_op jit(solution)/shard_map/all_gather | solution.py:114
  526.1 9.6 fusion.110
  559.9 9.1 multiply_convert_fusion.4
  583.8 10.7 fusion.39
  594.5 9.7 fusion.41
  611.5 12.3 add_convert_fusion
  642.1 30.1 %reduce-scatter.12.cloned.1.call-done = bf16[128,2080]{1,0:T(8,128)(2,1)} async-done(((bf16[512,2080]{1,0:T(8,128)(2,1)}), bf16[128,2080]{1,0:T(8,128)(2,1)}) %reduce-scatter.12.cloned.1.call-update) | async-done | bytes 532496 | tf_op jit(solution)/shard_map/reduce_scatter | solution.py:207
  677.6 40.4 %reduce-scatter.10.cloned.1.call-done = bf16[128,2048]{1,0:T(8,128)(2,1)} async-done(((bf16[512,2048]{1,0:T(8,128)(2,1)}), bf16[128,2048]{1,0:T(8,128)(2,1)}) %reduce-scatter.10.cloned.1.call-update) | async-done | bytes 524304 | tf_op jit(solution)/shard_map/reduce_scatter | solution.py:215
  737.4 14.1 all-to-all-done.1
  768.3 9.8 fusion.8
  806.8 9.1 pad_maximum_fusion.3
  826.3 9.1 pad_maximum_fusion.2
  845.9 9.1 pad_maximum_fusion.1
  865.3 9.0 pad_maximum_fusion
  875.6 35.4 %reduce-scatter.14.cloned.1.call-done = bf16[128,2048]{1,0:T(8,128)(2,1)} async-done(((bf16[512,2048]{1,0:T(8,128)(2,1)}), bf16[128,2048]{1,0:T(8,128)(2,1)}) %reduce-scatter.14.cloned.1.call-update) | async-done | bytes 524304 | tf_op jit(solution)/shard_map/reduce_scatter | solution.py:262
  914.8 49.5 %all-reduce.9.cloned.1.call-done = bf16[256,2048]{1,0:T(8,128)(2,1)} async-done(((bf16[256,2048]{1,0:T(8,128)(2,1)}), bf16[256,2048]{1,0:T(8,128)(2,1)}) %all-reduce.9.cloned.1.call-update) | async-done | bytes 1048592 | tf_op jit(solution)/shard_map/psum | solution.py:243
  967.1 92.2 %reduce-scatter.26.cloned.1.call-done = bf16[1,384,2048]{2,1,0:T(8,128)(2,1)} async-done(((bf16[8,384,2048]{2,1,0:T(8,128)(2,1)}), bf16[1,384,2048]{2,1,0:T(8,128)(2,1)}) %reduce-scatter.26.cloned.1.call-update) | async-done | bytes 1572880 | tf_op jit(solution)/shard_map/reduce_scatter | solution.py:196
  1061.1 93.8 %reduce-scatter.24.cloned.1.call-done = bf16[1,384,2048]{2,1,0:T(8,128)(2,1)} async-done(((bf16[8,384,2048]{2,1,0:T(8,128)(2,1)}), bf16[1,384,2048]{2,1,0:T(8,128)(2,1)}) %reduce-scatter.24.cloned.1.call-update) | async-done | bytes 1572880 | tf_op jit(solution)/shard_map/reduce_scatter | solution.py:196
  1158.9 91.7 %reduce-scatter.22.cloned.1.call-done = bf16[1,384,2048]{2,1,0:T(8,128)(2,1)} async-done(((bf16[8,384,2048]{2,1,0:T(8,128)(2,1)}), bf16[1,384,2048]{2,1,0:T(8,128)(2,1)}) %reduce-scatter.22.cloned.1.call-update) | async-done | bytes 1572880 | tf_op jit(solution)/shard_map/reduce_scatter | solution.py:196
  1254.6 91.8 %reduce-scatter.20.cloned.1.call-done = bf16[1,384,2048]{2,1,0:T(8,128)(2,1)} async-done(((bf16[8,384,2048]{2,1,0:T(8,128)(2,1)}), bf16[1,384,2048]{2,1,0:T(8,128)(2,1)}) %reduce-scatter.20.cloned.1.call-update) | async-done | bytes 1572880 | tf_op jit(solution)/shard_map/reduce_scatter | solution.py:196
  1356.2 59.4 %all-gather.37.cloned.1.call-done = bf16[1024,1664]{0,1:T(8,128)(2,1)} async-done(((bf16[256,1664]{0,1:T(8,128)(2,1)}), bf16[1024,1664]{0,1:T(8,128)(2,1)}) %all-gather.37.cloned.1.call-update) | async-done | bytes 3407888 | tf_op jit(solution)/shard_map/all_gather | solution.py:290
  1433.3 8.7 copy.187
  (411 shorter events, 327.3 us)
Async XLA Ops:
  7.2 50.8 %all-gather.25.cloned.1.call-start = ((), (), s32[]{:S(2)}) async-start(), calls=%async_computation.24 | async-start | bytes 2621440 | tf_op jit(solution)/shard_map/all_gather | solution.py:94
  7.9 100.2 %all-gather.19.cloned.1.call-start = ((), (), s32[]{:S(2)}) async-start(), calls=%async_computation.11 | async-start | bytes 7667712 | tf_op jit(solution)/shard_map/all_gather | solution.py:110
  13.8 94.4 %copy-start.73 = (bf16[8,128]{1,0:T(8,128)(2,1)S(1)}, bf16[8,128]{1,0:T(8,128)(2,1)}, u32[]{:S(2)}) copy-start(bf16[8,128]{1,0:T(8,128)(2,1)} %constant.61.clone) | copy-start | bytes 6148
  14.9 149.4 %all-gather.21.cloned.1.call-start = ((), (), s32[]{:S(2)}) async-start(), calls=%async_computation.12 | async-start | bytes 9437184 | tf_op jit(solution)/shard_map/all_gather | solution.py:111
  15.7 201.6 %all-gather.23.cloned.1.call-start = ((), (), s32[]{:S(2)}) async-start(), calls=%async_computation.13 | async-start | bytes 2621440 | tf_op jit(solution)/shard_map/all_gather | solution.py:155
  18.4 106.9 %copy-start.28 = (f32[512,64]{1,0:T(8,128)}, f32[512,64]{1,0:T(8,128)S(1)}, u32[]{:S(2)}) copy-start(f32[512,64]{1,0:T(8,128)S(1)} %get-tuple-element.77) | copy-start | bytes 393220
  60.1 49.4 %copy-start.74 = (f32[512]{0:T(512)}, f32[512]{0:T(512)S(1)}, u32[]{:S(2)}) copy-start(f32[512]{0:T(512)S(1)} %add_rsqrt_fusion.2) | copy-start | bytes 6148
  109.5 59.8 %copy-start.53 = (f32[1,2048]{1,0:T(1,128)}, f32[1,2048]{1,0:T(1,128)S(1)}, u32[]{:S(2)}) copy-start(f32[1,2048]{1,0:T(1,128)S(1)} %get-tuple-element.73) | copy-start | bytes 24580
  171.2 119.2 %all-gather.31.cloned.1.call-start = ((), (), s32[]{:S(2)}) async-start(), calls=%async_computation.27 | async-start | bytes 14155776 | tf_op jit(solution)/shard_map/all_gather | solution.py:114
  175.8 189.0 %all-gather.27.cloned.1.call-start = ((), (), s32[]{:S(2)}) async-start(), calls=%async_computation.25 | async-start | bytes 14155776 | tf_op jit(solution)/shard_map/all_gather | solution.py:114
  178.2 260.5 %all-gather.29.cloned.1.call-start = ((), (), s32[]{:S(2)}) async-start(), calls=%async_computation.26 | async-start | bytes 14155776 | tf_op jit(solution)/shard_map/all_gather | solution.py:114
  180.8 331.8 %all-gather.33.cloned.1.call-start = ((), (), s32[]{:S(2)}) async-start(), calls=%async_computation.28 | async-start | bytes 14155776 | tf_op jit(solution)/shard_map/all_gather | solution.py:114
  182.1 377.8 %all-gather.35.cloned.1.call-start = ((), (), s32[]{:S(2)}) async-start(), calls=%async_computation.29 | async-start | bytes 2621440 | tf_op jit(solution)/shard_map/all_gather | solution.py:112
  182.8 489.3 %reduce-scatter.12.cloned.1.call-start = ((), (), s32[]{:S(2)}) async-start(), calls=%async_computation.15 | async-start | bytes 2785280 | tf_op jit(solution)/shard_map/reduce_scatter | solution.py:207
  197.0 101.9 %copy-start.49 = (pred[512,16]{1,0:T(8,128)(4,1)}, pred[512,16]{1,0:T(8,128)(4,1)S(1)}, u32[]{:S(2)}) copy-start(pred[512,16]{1,0:T(8,128)(4,1)S(1)} %copy.167) | copy-start | bytes 24580
  220.2 78.6 %copy-start.64 = (f32[512]{0:T(512)}, f32[512]{0:T(512)S(1)}, u32[]{:S(2)}) copy-start(f32[512]{0:T(512)S(1)} %get-tuple-element.25) | copy-start | bytes 6148
  583.2 53.8 %copy-start.78 = (bf16[512,1024]{1,0:T(8,128)(2,1)}, bf16[512,1024]{1,0:T(8,128)(2,1)S(1)}, u32[]{:S(2)}) copy-start(bf16[512,1024]{1,0:T(8,128)(2,1)S(1)} %get-tuple-element.39) | copy-start | bytes 3145732
  626.7 91.3 %reduce-scatter.10.cloned.1.call-start = ((), (), s32[]{:S(2)}) async-start(), calls=%async_computation.14 | async-start | bytes 2621440 | tf_op jit(solution)/shard_map/reduce_scatter | solution.py:215
  637.0 37.4 %copy-start.46 = (f32[512,16]{1,0:T(8,128)S(1)}, f32[512,16]{1,0:T(8,128)}, u32[]{:S(2)}) copy-start(f32[512,16]{1,0:T(8,128)} %copy-done.45) | copy-start | bytes 98308
  640.8 34.6 %copy-start.71 = (f32[128]{0:T(128)S(1)}, f32[128]{0:T(128)}, u32[]{:S(2)}) copy-start(f32[128]{0:T(128)} %copy-done.70) | copy-start | bytes 1540
  640.8 77.2 %copy-start.35 = (bf16[1,128,2048]{2,1,0:T(8,128)(2,1)S(1)}, bf16[1,128,2048]{2,1,0:T(8,128)(2,1)}, u32[]{:S(2)}) copy-start(bf16[1,128,2048]{2,1,0:T(8,128)(2,1)} %param.15) | copy-start | bytes 1572868
  640.9 156.3 %reduce-scatter.18.cloned.1.call-start = ((), (), s32[]{:S(2)}) async-start(), calls=%async_computation.18 | async-start | bytes 9437184 | tf_op jit(solution)/shard_map/reduce_scatter | solution.py:240
  674.3 46.2 %copy-start.9 = (bf16[128,4,4,128]{0,3,2,1:T(8,128)(2,1)S(1)}, bf16[128,4,4,128]{0,3,2,1:T(8,128)(2,1)}, u32[]{:S(2)}) copy-start(bf16[128,4,4,128]{0,3,2,1:T(8,128)(2,1)} %copy-done.8) | copy-start | bytes 1572868
  733.6 17.9 %all-to-all-start.1 = ((bf16[128,16,128]{2,0,1:T(8,128)(2,1)}), bf16[128,16,128]{2,0,1:T(8,128)(2,1)S(1)}, u32[]{:S(2)}, u32[]{:S(2)}) async-start(bf16[128,16,128]{2,0,1:T(8,128)(2,1)} %bitcast.275), calls=%async_computation.3 | async-start | bytes 1048576 | tf_op jit(solution)/shard_map/all_to_all | solution.py:238
  737.1 137.4 %reduce-scatter.16.cloned.1.call-start = ((), (), s32[]{:S(2)}) async-start(), calls=%async_computation.17 | async-start | bytes 7667712 | tf_op jit(solution)/shard_map/reduce_scatter | solution.py:284
  791.9 119.1 %reduce-scatter.14.cloned.1.call-start = ((), (), s32[]{:S(2)}) async-start(), calls=%async_computation.16 | async-start | bytes 2621440 | tf_op jit(solution)/shard_map/reduce_scatter | solution.py:262
  792.5 171.9 %all-reduce.9.cloned.1.call-start = ((), (), s32[]{:S(2)}) async-start(), calls=%async_computation.19 | async-start | bytes 2097152 | tf_op jit(solution)/shard_map/psum | solution.py:243
  797.2 262.1 %reduce-scatter.26.cloned.1.call-start = ((), (), s32[]{:S(2)}) async-start(), calls=%async_computation.23 | async-start | bytes 14155776 | tf_op jit(solution)/shard_map/reduce_scatter | solution.py:196
  815.9 339.1 %reduce-scatter.24.cloned.1.call-start = ((), (), s32[]{:S(2)}) async-start(), calls=%async_computation.22 | async-start | bytes 14155776 | tf_op jit(solution)/shard_map/reduce_scatter | solution.py:196
  835.4 415.2 %reduce-scatter.22.cloned.1.call-start = ((), (), s32[]{:S(2)}) async-start(), calls=%async_computation.21 | async-start | bytes 14155776 | tf_op jit(solution)/shard_map/reduce_scatter | solution.py:196
  855.0 491.5 %reduce-scatter.20.cloned.1.call-start = ((), (), s32[]{:S(2)}) async-start(), calls=%async_computation.20 | async-start | bytes 14155776 | tf_op jit(solution)/shard_map/reduce_scatter | solution.py:196
  874.4 541.2 %all-gather.37.cloned.1.call-start = ((), (), s32[]{:S(2)}) async-start(), calls=%async_computation.30 | async-start | bytes 4259840 | tf_op jit(solution)/shard_map/all_gather | solution.py:290
  (95 other events, 575.3 us)
Sparse Core Ops, SparseCore 0:
  9.6 48.3 all-gather.24
  60.4 47.6 all-gather.18
  110.1 54.2 all-gather.20
  171.3 45.9 all-gather.22
  219.6 70.7 all-gather.30
  292.7 71.9 all-gather.26
  366.7 71.9 all-gather.28
  440.6 71.9 all-gather.32
  514.2 45.6 all-gather.34
  626.8 45.2 reduce-scatter.11
  675.0 42.9 reduce-scatter.9
  726.4 70.6 reduce-scatter.17
  800.6 64.0 reduce-scatter.15
  867.4 43.6 reduce-scatter.13
  913.2 51.0 all-reduce.8
  967.7 91.5 reduce-scatter.25
  1062.6 92.2 reduce-scatter.23
  1158.3 92.2 reduce-scatter.21
  1254.1 92.2 reduce-scatter.19
  1347.9 67.6 all-gather.36
where the time goes:
time: 1470 us; the launch traced here: 1460 us
  waiting for transfers between devices  979 us (67%)
  matrix products  200 us (14%)
  local copies, waits for them, and re-layouts  134 us (9%)
  other arithmetic  88.7 us (6%)
  blocking collectives  33.2 us (2%)
  between operations  16 us (1%)
    reduce_scatter x4, waiting for transfers between devices, body(): lax.psum_scatter(joined, 'wt', scatter_dimension=0, tiled=False).astype(F32)  369 us
    all_gather x4, waiting for transfers between devices, body(): lax.all_gather(jnp.concatenate([w_gate_up[e], w_down[e]], axis=0), 'wt',...  249 us
    dot_general x34, matrix products, dot(): lax.dot_general(left, right, (dims, ((), ())), preferred_element_type=F32)  188 us
    all_gather x1, waiting for transfers between devices, body(): collected = lax.all_gather(scattered, 'seq', axis=0).astype(F32)  59.4 us
    psum x1, waiting for transfers between devices, body(): out_grad = lax.psum(out_grad, 'seq').astype(F32)  49.5 us
    all_gather x1, waiting for transfers between devices, body(): lax.all_gather(jnp.concatenate([w_here, small], axis=1), 'wt', axis=0, ti...  48.1 us
    reduce_scatter x1, waiting for transfers between devices, body(): lax.psum_scatter(out_part.astype(BF), 'seq', scatter_dimension=0, tiled=T...  40.4 us
    all_gather x1, waiting for transfers between devices, body(): tokens_all = lax.all_gather(tokens[0], 'seq', axis=0, tiled=True)  39.6 us
  transfers between devices with their start and end apart: 21, of which 20 were waited for; matrix products, arithmetic and copies ran while one was open for 20% of the time, Pallas kernels for 0%

commit v1 on v0

--- a/solution.py
+++ b/solution.py
@@ -240,7 +240,7 @@
     out_grad = lax.psum_scatter(
         tn(merged, grad_branch).astype(BF), "wt", scatter_dimension=0, tiled=True
     )
-    out_grad = lax.psum(out_grad, "seq").astype(F32)
+    out_grad = jnp.sum(lax.all_gather(out_grad, "seq"), axis=0).astype(F32)
     grad_weights = bmm(grad_heads, values, ((2,), (2,)))
     inner = jnp.sum(weights * grad_weights, axis=-1, keepdims=True)
     grad_scores = (weights * (grad_weights - inner)).astype(BF)

time: 1470 us -> 1520 us (1.034)
  waiting for transfers between devices: 979 us -> 1030 us
    psum x1 -> x0, waiting for transfers between devices: 49.5 us -> none  [body(): out_grad = lax.psum(out_grad, 'seq').astype(F32)]
    reduce_scatter x1, waiting for transfers between devices: 4.6 us -> 52 us  [body(): lax.psum_scatter(tn(merged, grad_branch).astype(BF), 'wt', scatter_dimens...]
    all_gather x0 -> x1, waiting for transfers between devices: none -> 45.6 us  [body(): out_grad = jnp.sum(lax.all_gather(out_grad, 'seq'), axis=0).astype(F32)]
  transfers between devices with their start and end apart: 21 -> 21, of which waited for: 20 -> 20; matrix products, arithmetic and copies ran while one was open for 20% -> 19% of each run, Pallas kernels for 0% -> 0%
where the time goes in v1:
time: 1520 us; the launch traced here: 1510 us
  waiting for transfers between devices  1030 us (68%)
  matrix products  200 us (13%)
  local copies, waits for them, and re-layouts  135 us (9%)
  other arithmetic  90.5 us (6%)
  blocking collectives  33.2 us (2%)
  between operations  16 us (1%)
    reduce_scatter x4, waiting for transfers between devices, body(): lax.psum_scatter(joined, 'wt', scatter_dimension=0, tiled=False).astype(F32)  368 us
    all_gather x4, waiting for transfers between devices, body(): lax.all_gather(jnp.concatenate([w_gate_up[e], w_down[e]], axis=0), 'wt',...  249 us
    dot_general x34, matrix products, dot(): lax.dot_general(left, right, (dims, ((), ())), preferred_element_type=F32)  187 us
    all_gather x1, waiting for transfers between devices, body(): collected = lax.all_gather(scattered, 'seq', axis=0).astype(F32)  59.6 us
    reduce_scatter x1, waiting for transfers between devices, body(): lax.psum_scatter(tn(merged, grad_branch).astype(BF), 'wt', scatter_dimens...  52 us
    all_gather x1, waiting for transfers between devices, body(): lax.all_gather(jnp.concatenate([w_here, small], axis=1), 'wt', axis=0, ti...  48.1 us
    reduce_scatter x1, waiting for transfers between devices, body(): lax.psum_scatter(grad_normed_part.astype(BF), 'seq', scatter_dimension=0,...  46.1 us
    all_gather x1, waiting for transfers between devices, body(): out_grad = jnp.sum(lax.all_gather(out_grad, 'seq'), axis=0).astype(F32)  45.6 us
  transfers between devices with their start and end apart: 21, of which 20 were waited for; matrix products, arithmetic and copies ran while one was open for 19% of the time, Pallas kernels for 0%

profile of v1, /device:TPU:0, one launch (start us, length us, event | category | flops | bytes accessed | tf_op | source)
XLA Modules:
  0.0 1514.1 jit_solution(11690220598688854822)
XLA Ops:
  18.4 39.6 %all-gather.27.cloned.1.call-done = bf16[1,512,2048]{2,1,0:T(8,128)(2,1)} async-done(((bf16[1,128,2048]{2,1,0:T(8,128)(2,1)}), bf16[1,512,2048]{2,1,0:T(8,128)(2,1)}) %all-gather.27.cloned.1.call-update) | async-done | bytes 2097168 | tf_op jit(solution)/shard_map/all_gather | solution.py:94
  60.1 48.1 %all-gather.21.cloned.1.call-done = bf16[2048,1664]{0,1:T(8,128)(2,1)} async-done(((bf16[256,1664]{0,1:T(8,128)(2,1)}), bf16[2048,1664]{0,1:T(8,128)(2,1)}) %all-gather.21.cloned.1.call-update) | async-done | bytes 6815760 | tf_op jit(solution)/shard_map/all_gather | solution.py:110
  110.0 8.6 fusion.3
  133.8 19.4 %all_to_all.33 = bf16[512,4,128]{2,1,0:T(4,128)(2,1)S(1)} all-to-all(bf16[512,4,128]{2,1,0:T(4,128)(2,1)S(1)} %copy.163), channel_id=1, replica_groups=mesh['seq'=4,'wt'=8] {'seq'}, dimensions={0} | all-to-all | bytes 1048576 | tf_op jit(solution)/shard_map/all_to_all | solution.py:148
  153.5 10.9 all-gather.23.cloned.1.call-done
  182.9 13.9 all-gather.1
  197.0 20.3 %all-gather.25.cloned.1.call-done = bf16[512,2048]{1,0:T(8,128)(2,1)} async-done(((bf16[128,2048]{1,0:T(8,128)(2,1)}), bf16[512,2048]{1,0:T(8,128)(2,1)}) %all-gather.25.cloned.1.call-update) | async-done | bytes 2097168 | tf_op jit(solution)/shard_map/all_gather | solution.py:155
  222.5 68.0 %all-gather.33.cloned.1.call-done = bf16[3072,2048]{1,0:T(8,128)(2,1)} async-done(((bf16[384,2048]{1,0:T(8,128)(2,1)}), bf16[3072,2048]{1,0:T(8,128)(2,1)}) %all-gather.33.cloned.1.call-update) | async-done | bytes 12582928 | tf_op jit(solution)/shard_map/all_gather | solution.py:114
  304.3 60.5 %all-gather.29.cloned.1.call-done = bf16[3072,2048]{1,0:T(8,128)(2,1)} async-done(((bf16[384,2048]{1,0:T(8,128)(2,1)}), bf16[3072,2048]{1,0:T(8,128)(2,1)}) %all-gather.29.cloned.1.call-update) | async-done | bytes 12582928 | tf_op jit(solution)/shard_map/all_gather | solution.py:114
  378.5 60.2 %all-gather.31.cloned.1.call-done = bf16[3072,2048]{1,0:T(8,128)(2,1)} async-done(((bf16[384,2048]{1,0:T(8,128)(2,1)}), bf16[3072,2048]{1,0:T(8,128)(2,1)}) %all-gather.31.cloned.1.call-update) | async-done | bytes 12582928 | tf_op jit(solution)/shard_map/all_gather | solution.py:114
  452.5 60.1 %all-gather.35.cloned.1.call-done = bf16[3072,2048]{1,0:T(8,128)(2,1)} async-done(((bf16[384,2048]{1,0:T(8,128)(2,1)}), bf16[3072,2048]{1,0:T(8,128)(2,1)}) %all-gather.35.cloned.1.call-update) | async-done | bytes 12582928 | tf_op jit(solution)/shard_map/all_gather | solution.py:114
  526.1 9.6 fusion.110
  559.9 9.1 multiply_convert_fusion.4
  583.8 10.7 fusion.39
  594.6 9.7 fusion.41
  611.4 12.3 add_convert_fusion
  641.7 30.3 %reduce-scatter.12.cloned.1.call-done = bf16[128,2080]{1,0:T(8,128)(2,1)} async-done(((bf16[512,2080]{1,0:T(8,128)(2,1)}), bf16[128,2080]{1,0:T(8,128)(2,1)}) %reduce-scatter.12.cloned.1.call-update) | async-done | bytes 532496 | tf_op jit(solution)/shard_map/reduce_scatter | solution.py:207
  676.6 41.3 %reduce-scatter.10.cloned.1.call-done = bf16[128,2048]{1,0:T(8,128)(2,1)} async-done(((bf16[512,2048]{1,0:T(8,128)(2,1)}), bf16[128,2048]{1,0:T(8,128)(2,1)}) %reduce-scatter.10.cloned.1.call-update) | async-done | bytes 524304 | tf_op jit(solution)/shard_map/reduce_scatter | solution.py:215
  731.7 13.6 all-to-all-done.1
  762.1 9.6 fusion.8
  803.9 9.1 pad_maximum_fusion.3
  823.4 9.2 pad_maximum_fusion.2
  842.9 9.1 pad_maximum_fusion.1
  862.4 9.0 pad_maximum_fusion
  872.5 52.0 %reduce-scatter.18.cloned.1.call-done = bf16[256,2048]{1,0:T(8,128)(2,1)} async-done(((bf16[2048,2048]{1,0:T(8,128)(2,1)}), bf16[256,2048]{1,0:T(8,128)(2,1)}) %reduce-scatter.18.cloned.1.call-update) | async-done | bytes 1048592 | tf_op jit(solution)/shard_map/reduce_scatter | solution.py:240
  924.7 46.1 %reduce-scatter.14.cloned.1.call-done = bf16[128,2048]{1,0:T(8,128)(2,1)} async-done(((bf16[512,2048]{1,0:T(8,128)(2,1)}), bf16[128,2048]{1,0:T(8,128)(2,1)}) %reduce-scatter.14.cloned.1.call-update) | async-done | bytes 524304 | tf_op jit(solution)/shard_map/reduce_scatter | solution.py:262
  974.6 91.1 %reduce-scatter.26.cloned.1.call-done = bf16[1,384,2048]{2,1,0:T(8,128)(2,1)} async-done(((bf16[8,384,2048]{2,1,0:T(8,128)(2,1)}), bf16[1,384,2048]{2,1,0:T(8,128)(2,1)}) %reduce-scatter.26.cloned.1.call-update) | async-done | bytes 1572880 | tf_op jit(solution)/shard_map/reduce_scatter | solution.py:196
  1067.5 93.8 %reduce-scatter.24.cloned.1.call-done = bf16[1,384,2048]{2,1,0:T(8,128)(2,1)} async-done(((bf16[8,384,2048]{2,1,0:T(8,128)(2,1)}), bf16[1,384,2048]{2,1,0:T(8,128)(2,1)}) %reduce-scatter.24.cloned.1.call-update) | async-done | bytes 1572880 | tf_op jit(solution)/shard_map/reduce_scatter | solution.py:196
  1165.4 91.7 %reduce-scatter.22.cloned.1.call-done = bf16[1,384,2048]{2,1,0:T(8,128)(2,1)} async-done(((bf16[8,384,2048]{2,1,0:T(8,128)(2,1)}), bf16[1,384,2048]{2,1,0:T(8,128)(2,1)}) %reduce-scatter.22.cloned.1.call-update) | async-done | bytes 1572880 | tf_op jit(solution)/shard_map/reduce_scatter | solution.py:196
  1261.0 91.7 %reduce-scatter.20.cloned.1.call-done = bf16[1,384,2048]{2,1,0:T(8,128)(2,1)} async-done(((bf16[8,384,2048]{2,1,0:T(8,128)(2,1)}), bf16[1,384,2048]{2,1,0:T(8,128)(2,1)}) %reduce-scatter.20.cloned.1.call-update) | async-done | bytes 1572880 | tf_op jit(solution)/shard_map/reduce_scatter | solution.py:196
  1362.5 59.6 %all-gather.39.cloned.1.call-done = bf16[1024,1664]{0,1:T(8,128)(2,1)} async-done(((bf16[256,1664]{0,1:T(8,128)(2,1)}), bf16[1024,1664]{0,1:T(8,128)(2,1)}) %all-gather.39.cloned.1.call-update) | async-done | bytes 3407888 | tf_op jit(solution)/shard_map/all_gather | solution.py:290
  1456.8 45.6 %all-gather.41.cloned.1.call-done = bf16[1024,2048]{1,0:T(8,128)(2,1)} async-done(((bf16[256,2048]{1,0:T(8,128)(2,1)}), bf16[1024,2048]{1,0:T(8,128)(2,1)}) %all-gather.41.cloned.1.call-update) | async-done | bytes 4194320 | tf_op jit(solution)/shard_map/all_gather | solution.py:243
  (414 shorter events, 334.3 us)
Async XLA Ops:
  7.2 50.8 %all-gather.27.cloned.1.call-start = ((), (), s32[]{:S(2)}) async-start(), calls=%async_computation.23 | async-start | bytes 2621440 | tf_op jit(solution)/shard_map/all_gather | solution.py:94
  7.9 100.2 %all-gather.21.cloned.1.call-start = ((), (), s32[]{:S(2)}) async-start(), calls=%async_computation.11 | async-start | bytes 7667712 | tf_op jit(solution)/shard_map/all_gather | solution.py:110
  13.8 94.4 %copy-start.73 = (bf16[8,128]{1,0:T(8,128)(2,1)S(1)}, bf16[8,128]{1,0:T(8,128)(2,1)}, u32[]{:S(2)}) copy-start(bf16[8,128]{1,0:T(8,128)(2,1)} %constant.62.clone) | copy-start | bytes 6148
  14.9 149.4 %all-gather.23.cloned.1.call-start = ((), (), s32[]{:S(2)}) async-start(), calls=%async_computation.12 | async-start | bytes 9437184 | tf_op jit(solution)/shard_map/all_gather | solution.py:111
  15.7 201.7 %all-gather.25.cloned.1.call-start = ((), (), s32[]{:S(2)}) async-start(), calls=%async_computation.13 | async-start | bytes 2621440 | tf_op jit(solution)/shard_map/all_gather | solution.py:155
  18.4 106.9 %copy-start.28 = (f32[512,64]{1,0:T(8,128)}, f32[512,64]{1,0:T(8,128)S(1)}, u32[]{:S(2)}) copy-start(f32[512,64]{1,0:T(8,128)S(1)} %get-tuple-element.77) | copy-start | bytes 393220
  60.1 49.4 %copy-start.74 = (f32[512]{0:T(512)}, f32[512]{0:T(512)S(1)}, u32[]{:S(2)}) copy-start(f32[512]{0:T(512)S(1)} %add_rsqrt_fusion.2) | copy-start | bytes 6148
  109.5 59.8 %copy-start.53 = (f32[1,2048]{1,0:T(1,128)}, f32[1,2048]{1,0:T(1,128)S(1)}, u32[]{:S(2)}) copy-start(f32[1,2048]{1,0:T(1,128)S(1)} %get-tuple-element.73) | copy-start | bytes 24580
  171.2 119.2 %all-gather.33.cloned.1.call-start = ((), (), s32[]{:S(2)}) async-start(), calls=%async_computation.26 | async-start | bytes 14155776 | tf_op jit(solution)/shard_map/all_gather | solution.py:114
  175.8 189.0 %all-gather.29.cloned.1.call-start = ((), (), s32[]{:S(2)}) async-start(), calls=%async_computation.24 | async-start | bytes 14155776 | tf_op jit(solution)/shard_map/all_gather | solution.py:114
  178.2 260.5 %all-gather.31.cloned.1.call-start = ((), (), s32[]{:S(2)}) async-start(), calls=%async_computation.25 | async-start | bytes 14155776 | tf_op jit(solution)/shard_map/all_gather | solution.py:114
  180.8 331.8 %all-gather.35.cloned.1.call-start = ((), (), s32[]{:S(2)}) async-start(), calls=%async_computation.27 | async-start | bytes 14155776 | tf_op jit(solution)/shard_map/all_gather | solution.py:114
  182.1 377.8 %all-gather.37.cloned.1.call-start = ((), (), s32[]{:S(2)}) async-start(), calls=%async_computation.28 | async-start | bytes 2621440 | tf_op jit(solution)/shard_map/all_gather | solution.py:112
  182.9 489.2 %reduce-scatter.12.cloned.1.call-start = ((), (), s32[]{:S(2)}) async-start(), calls=%async_computation.15 | async-start | bytes 2785280 | tf_op jit(solution)/shard_map/reduce_scatter | solution.py:207
  197.0 101.9 %copy-start.49 = (pred[512,16]{1,0:T(8,128)(4,1)}, pred[512,16]{1,0:T(8,128)(4,1)S(1)}, u32[]{:S(2)}) copy-start(pred[512,16]{1,0:T(8,128)(4,1)S(1)} %copy.167) | copy-start | bytes 24580
  220.3 78.6 %copy-start.64 = (f32[512]{0:T(512)}, f32[512]{0:T(512)S(1)}, u32[]{:S(2)}) copy-start(f32[512]{0:T(512)S(1)} %get-tuple-element.25) | copy-start | bytes 6148
  583.3 53.7 %copy-start.77 = (bf16[512,1024]{1,0:T(8,128)(2,1)}, bf16[512,1024]{1,0:T(8,128)(2,1)S(1)}, u32[]{:S(2)}) copy-start(bf16[512,1024]{1,0:T(8,128)(2,1)S(1)} %get-tuple-element.39) | copy-start | bytes 3145732
  626.6 91.3 %reduce-scatter.10.cloned.1.call-start = ((), (), s32[]{:S(2)}) async-start(), calls=%async_computation.14 | async-start | bytes 2621440 | tf_op jit(solution)/shard_map/reduce_scatter | solution.py:215
  637.0 37.2 %copy-start.46 = (f32[512,16]{1,0:T(8,128)S(1)}, f32[512,16]{1,0:T(8,128)}, u32[]{:S(2)}) copy-start(f32[512,16]{1,0:T(8,128)} %copy-done.45) | copy-start | bytes 98308
  640.8 34.4 %copy-start.54 = (f32[1,2048]{1,0:T(1,128)S(1)}, f32[1,2048]{1,0:T(1,128)}, u32[]{:S(2)}) copy-start(f32[1,2048]{1,0:T(1,128)} %copy-done.53) | copy-start | bytes 24580
  640.8 34.4 %copy-start.71 = (f32[128]{0:T(128)S(1)}, f32[128]{0:T(128)}, u32[]{:S(2)}) copy-start(f32[128]{0:T(128)} %copy-done.70) | copy-start | bytes 1540
  727.5 17.8 %all-to-all-start.1 = ((bf16[128,16,128]{2,0,1:T(8,128)(2,1)}), bf16[128,16,128]{2,0,1:T(8,128)(2,1)S(1)}, u32[]{:S(2)}, u32[]{:S(2)}) async-start(bf16[128,16,128]{2,0,1:T(8,128)(2,1)} %bitcast.276), calls=%async_computation.3 | async-start | bytes 1048576 | tf_op jit(solution)/shard_map/all_to_all | solution.py:238
  731.0 140.6 %reduce-scatter.16.cloned.1.call-start = ((), (), s32[]{:S(2)}) async-start(), calls=%async_computation.17 | async-start | bytes 7667712 | tf_op jit(solution)/shard_map/reduce_scatter | solution.py:284
  785.6 138.9 %reduce-scatter.18.cloned.1.call-start = ((), (), s32[]{:S(2)}) async-start(), calls=%async_computation.18 | async-start | bytes 9437184 | tf_op jit(solution)/shard_map/reduce_scatter | solution.py:240
  793.0 177.9 %reduce-scatter.14.cloned.1.call-start = ((), (), s32[]{:S(2)}) async-start(), calls=%async_computation.16 | async-start | bytes 2621440 | tf_op jit(solution)/shard_map/reduce_scatter | solution.py:262
  793.6 272.1 %reduce-scatter.26.cloned.1.call-start = ((), (), s32[]{:S(2)}) async-start(), calls=%async_computation.22 | async-start | bytes 14155776 | tf_op jit(solution)/shard_map/reduce_scatter | solution.py:196
  813.0 348.4 %reduce-scatter.24.cloned.1.call-start = ((), (), s32[]{:S(2)}) async-start(), calls=%async_computation.21 | async-start | bytes 14155776 | tf_op jit(solution)/shard_map/reduce_scatter | solution.py:196
  832.6 424.5 %reduce-scatter.22.cloned.1.call-start = ((), (), s32[]{:S(2)}) async-start(), calls=%async_computation.20 | async-start | bytes 14155776 | tf_op jit(solution)/shard_map/reduce_scatter | solution.py:196
  852.1 500.7 %reduce-scatter.20.cloned.1.call-start = ((), (), s32[]{:S(2)}) async-start(), calls=%async_computation.19 | async-start | bytes 14155776 | tf_op jit(solution)/shard_map/reduce_scatter | solution.py:196
  871.5 53.1 %copy-start.7 = (bf16[1,128,2048]{2,1,0:T(8,128)(2,1)S(1)}, bf16[1,128,2048]{2,1,0:T(8,128)(2,1)}, u32[]{:S(2)}) copy-start(bf16[1,128,2048]{2,1,0:T(8,128)(2,1)} %param.14) | copy-start | bytes 1572868
  871.5 550.5 %all-gather.39.cloned.1.call-start = ((), (), s32[]{:S(2)}) async-start(), calls=%async_computation.29 | async-start | bytes 4259840 | tf_op jit(solution)/shard_map/all_gather | solution.py:290
  872.2 630.1 %all-gather.41.cloned.1.call-start = ((), (), s32[]{:S(2)}) async-start(), calls=%async_computation.30 | async-start | bytes 5242880 | tf_op jit(solution)/shard_map/all_gather | solution.py:243
  (96 other events, 519.4 us)
Sparse Core Ops, SparseCore 0:
  9.6 48.3 all-gather.26
  60.4 47.6 all-gather.20
  110.1 54.2 all-gather.22
  171.4 45.9 all-gather.24
  219.6 70.7 all-gather.32
  292.8 71.9 all-gather.28
  366.7 71.9 all-gather.30
  440.6 71.9 all-gather.34
  514.2 45.6 all-gather.36
  626.7 45.2 reduce-scatter.11
  674.9 42.9 reduce-scatter.9
  785.8 63.1 reduce-scatter.15
  852.9 71.5 reduce-scatter.17
  927.2 43.5 reduce-scatter.13
  974.2 91.4 reduce-scatter.25
  1069.1 92.2 reduce-scatter.23
  1164.7 92.2 reduce-scatter.21
  1260.4 92.2 reduce-scatter.19
  1354.3 67.6 all-gather.38
  1423.4 78.9 all-gather.40
